TPU v7x, 256 devices: a whole 4x4x8 slice. The times are simulated.
256 devices in a mesh: row: 32 (over y_lo, z, core), col: 8 (over y_hi, x).
Axes of the slice: x: 4, y: 4 (y_hi: 2, y_lo: 2; y = y_hi * 2 + y_lo), z: 8, core: 2. Of those that a mesh axis runs over, the one named last changes fastest.
Arguments:
- embeddings: bfloat16 [491520, 768], P(('row', 'col')), may hold values from -1 to 1, as said below
- valid: int32 [491520], P(('row', 'col')), may hold values 0 or 1
Outputs:
- best_match: float32 [491520], P(('row', 'col'))
- near_count: float32 [491520], P(('row', 'col'))
Inputs may be any that keep to these rules, and one draw needn't show every extreme that they name: `embeddings`: each row has length 1 up to bfloat16 rounding.
All inputs are finite; a program needn't handle non-finite values. No bound on the sum of `valid` on one device may be relied on, other than what follows from the above.
Results may differ from a plain program's by a relative error of at most 0.01.
Values may be sent and summed in bfloat16 or wider, within the bound.
A program may use at most 64 MiB of HBM per device.

v0:
```python
import jax
import jax.numpy as jnp
from jax import lax
from jax.sharding import PartitionSpec as P

STEPS = 3


THRESHOLD = 0.6
SHARPNESS = 0.05


def as_sent(value):

    def short(part):
        return part.astype(jnp.bfloat16) if part.dtype == jnp.float32 else part

    return jax.tree.map(short, value)


def shifted(value, axis, steps):
    count = lax.axis_size(axis)
    pairs = [(source, (source + steps) % count) for source in range(count)]
    return lax.ppermute(value, axis, pairs)


def tally(best, count, query, cand, cand_valid, own):
    scores = lax.dot_general(
        query, cand, (((1,), (1,)), ((), ())), preferred_element_type=jnp.float32
    )
    allowed = cand_valid[None, :] > 0
    if own:
        rows = jnp.arange(query.shape[0], dtype=jnp.int32)
        allowed = allowed & (rows[:, None] != rows[None, :])
    best = jnp.maximum(best, jnp.max(jnp.where(allowed, scores, -1.0), axis=1))
    soft = jax.nn.sigmoid((scores - THRESHOLD) / SHARPNESS)
    count = count + jnp.sum(jnp.where(allowed, soft, 0.0), axis=1)
    return (best, count)


def shards(embeddings, valid):
    members = embeddings.shape[0]
    best = jnp.full((members,), -1.0, jnp.float32)
    count = jnp.zeros((members,), jnp.float32)
    cand, cand_valid = (embeddings, valid)
    for step in range(STEPS):
        if step + 1 < STEPS:
            upper = (
                shifted(cand, "row", 1),
                shifted(as_sent(cand_valid), "row", 1).astype(cand_valid.dtype),
            )
            following = shifted((upper[0], as_sent(upper[1])), "col", -1)
        best, count = tally(best, count, embeddings, cand, cand_valid, step == 0)
        if step + 1 < STEPS:
            cand, cand_valid = following
    return (best, count)


def solution(mesh):
    return jax.shard_map(
        shards,
        mesh=mesh,
        in_specs=(P(("row", "col"), None), P(("row", "col"))),
        out_specs=(P(("row", "col")), P(("row", "col"))),
        check_vma=False,
    )
```

profile of v0, /device:TPU:6, one launch (start us, length us, event | category | flops | bytes accessed | tf_op | source)
XLA Modules:
  0.0 218.5 jit_solution(8164774922318225624)
XLA Ops:
  0.6 0.1 collective-permute-start.2
  0.7 39.4 %collective-permute-done.2 = bf16[1920,768]{1,0:T(8,128)(2,1)S(1)} collective-permute-done((bf16[1920,768]{1,0:T(8,128)(2,1)}, bf16[1920,768]{1,0:T(8,128)(2,1)S(1)}, u32[]{:S(2)}, u32[]{:S(2)}) %collective-permute-start.2) | collective-permute-done | bytes 2949152 | tf_op jit(solution)/shard_map/ppermute | solution.py:24
  40.1 0.8 collective-permute-start.3
  40.9 0.0 collective-permute-start
  40.9 5.5 %collective-permute-done = s32[1920]{0:T(1024)S(1)} collective-permute-done((s32[1920]{0:T(1024)}, s32[1920]{0:T(1024)S(1)}, u32[]{:S(2)}, u32[]{:S(2)}) %collective-permute-start) | collective-permute-done | bytes 7712 | tf_op jit(solution)/shard_map/ppermute | solution.py:24
  46.4 0.5 collective-permute-start.1
  46.8 0.7 broadcast_compare_fusion.2
  47.5 0.0 copy-start
  47.5 57.6 %collective-permute-done.1 = s32[1920]{0:T(1024)S(1)} collective-permute-done((s32[1920]{0:T(1024)S(1)}, s32[1920]{0:T(1024)S(1)}, u32[]{:S(2)}, u32[]{:S(2)}) %collective-permute-start.1) | collective-permute-done | bytes 7712 | tf_op jit(solution)/shard_map/ppermute | solution.py:24
  105.2 0.0 collective-permute-start.4
  105.2 0.0 collective-permute-done.3
  105.2 1.6 collective-permute-start.6
  106.8 14.1 %select_reduce_fusion.2 = (f32[1920]{0:T(1024)S(1)}, f32[1920]{0:T(1024)S(1)}) fusion(pred[1920]{0:T(1024)(128)(4,1)S(1)} %broadcast_compare_fusion.2, bf16[1920,768]{1,0:T(8,128)(2,1)} %param.2), kind=kOutput, calls=%fused_computation.2 | convolution fusion | flops 5702856704 | bytes 2966400 | tf_op jit(solution)/shard_map/dot_general | solution.py:28
  120.8 0.0 collective-permute-done.4
  120.9 0.1 collective-permute-start.5
  121.0 7.4 %collective-permute-done.5 = s32[1920]{0:T(1024)S(1)} collective-permute-done((s32[1920]{0:T(1024)S(1)}, s32[1920]{0:T(1024)S(1)}, u32[]{:S(2)}, u32[]{:S(2)}) %collective-permute-start.5) | collective-permute-done | bytes 7712 | tf_op jit(solution)/shard_map/ppermute | solution.py:24
  128.4 13.7 %collective-permute-done.6 = bf16[1920,768]{1,0:T(8,128)(2,1)S(1)} collective-permute-done((bf16[1920,768]{1,0:T(8,128)(2,1)S(1)}, bf16[1920,768]{1,0:T(8,128)(2,1)S(1)}, u32[]{:S(2)}, u32[]{:S(2)}) %collective-permute-start.6) | collective-permute-done | bytes 2949152 | tf_op jit(solution)/shard_map/ppermute | solution.py:24
  142.1 0.0 collective-permute-start.7
  142.1 0.0 copy-done
  142.1 9.5 %select_reduce_fusion.1 = (f32[1920]{0:T(1024)S(1)}, f32[1920]{0:T(1024)S(1)}) fusion(pred[1920]{0:T(1024)(128)(4,1)S(1)} %broadcast_compare_fusion.1, bf16[1920,768]{1,0:T(8,128)(2,1)S(1)} %copy-done, bf16[1920,768]{1,0:T(8,128)(2,1)S(1)} %collective-permute-done.3), kind=kOutput, calls=%fused_computation.1 | convolution fusion | flops 5695483904 | bytes 5915520 | tf_op jit(solution)/shard_map/dot_general | solution.py:28
  151.7 56.7 %collective-permute-done.7 = bf16[1920,768]{1,0:T(8,128)(2,1)S(1)} collective-permute-done((bf16[1920,768]{1,0:T(8,128)(2,1)S(1)}, bf16[1920,768]{1,0:T(8,128)(2,1)S(1)}, u32[]{:S(2)}, u32[]{:S(2)}) %collective-permute-start.7) | collective-permute-done | bytes 2949152 | tf_op jit(solution)/shard_map/ppermute | solution.py:24
  208.4 9.5 %select_reduce_fusion = (f32[1920]{0:T(1024)S(1)}, f32[1920]{0:T(1024)S(1)}) fusion(pred[1920]{0:T(1024)(128)(4,1)S(1)} %broadcast_compare_fusion, bf16[1920,768]{1,0:T(8,128)(2,1)S(1)} %copy-done, bf16[1920,768]{1,0:T(8,128)(2,1)S(1)} %collective-permute-done.7), kind=kOutput, calls=%fused_computation | convolution fusion | flops 5695483904 | bytes 5915520 | tf_op jit(solution)/shard_map/dot_general | solution.py:28
  217.9 0.6 add_add_fusion
  (2 shorter events, 0.0 us)
Async XLA Ops:
  0.6 39.4 %collective-permute-start.2 = (bf16[1920,768]{1,0:T(8,128)(2,1)}, bf16[1920,768]{1,0:T(8,128)(2,1)S(1)}, u32[]{:S(2)}, u32[]{:S(2)}) collective-permute-start(bf16[1920,768]{1,0:T(8,128)(2,1)} %param.2), channel_id=1, source_target_pairs={{0,8},{8,16},{16,24},{24,32},{32,40},{40,48},{48,56},{56,64},{64,7... | collective-permute-start | bytes 8847368 | tf_op jit(solution)/shard_map/ppermute | solution.py:24
  40.1 65.1 %collective-permute-start.3 = (bf16[1920,768]{1,0:T(8,128)(2,1)S(1)}, bf16[1920,768]{1,0:T(8,128)(2,1)S(1)}, u32[]{:S(2)}, u32[]{:S(2)}) collective-permute-start(bf16[1920,768]{1,0:T(8,128)(2,1)S(1)} %collective-permute-done.2), channel_id=1, source_target_pairs={{0,7},{1,0},{2,1},{3,2},{4,3},{5,4},{6,5},{7,6},{8,15},{9,8},{10,9... | collective-permute-start | bytes 8847368 | tf_op jit(solution)/shard_map/ppermute | solution.py:24
  40.9 5.5 %collective-permute-start = (s32[1920]{0:T(1024)}, s32[1920]{0:T(1024)S(1)}, u32[]{:S(2)}, u32[]{:S(2)}) collective-permute-start(s32[1920]{0:T(1024)} %param.3), channel_id=1, source_target_pairs={{0,8},{8,16},{16,24},{24,32},{32,40},{40,48},{48,56},{56,64},{64,7... | collective-permute-start | bytes 23048 | tf_op jit(solution)/shard_map/ppermute | solution.py:24
  46.4 58.8 %collective-permute-start.1 = (s32[1920]{0:T(1024)S(1)}, s32[1920]{0:T(1024)S(1)}, u32[]{:S(2)}, u32[]{:S(2)}) collective-permute-start(s32[1920]{0:T(1024)S(1)} %collective-permute-done), channel_id=1, source_target_pairs={{0,7},{1,0},{2,1},{3,2},{4,3},{5,4},{6,5},{7,6},{8,15},{9,8},{10,9... | collective-permute-start | bytes 23048 | tf_op jit(solution)/shard_map/ppermute | solution.py:24
  47.5 94.6 %copy-start = (bf16[1920,768]{1,0:T(8,128)(2,1)S(1)}, bf16[1920,768]{1,0:T(8,128)(2,1)}, u32[]{:S(2)}) copy-start(bf16[1920,768]{1,0:T(8,128)(2,1)} %param.2) | copy-start | bytes 8847364
  105.2 15.7 %collective-permute-start.4 = (s32[1920]{0:T(1024)S(1)}, s32[1920]{0:T(1024)S(1)}, u32[]{:S(2)}, u32[]{:S(2)}) collective-permute-start(s32[1920]{0:T(1024)S(1)} %collective-permute-done.1), channel_id=1, source_target_pairs={{0,8},{8,16},{16,24},{24,32},{32,40},{40,48},{48,56},{56,64},{64,7... | collective-permute-start | bytes 23048 | tf_op jit(solution)/shard_map/ppermute | solution.py:24
  105.2 37.0 %collective-permute-start.6 = (bf16[1920,768]{1,0:T(8,128)(2,1)S(1)}, bf16[1920,768]{1,0:T(8,128)(2,1)S(1)}, u32[]{:S(2)}, u32[]{:S(2)}) collective-permute-start(bf16[1920,768]{1,0:T(8,128)(2,1)S(1)} %collective-permute-done.3), channel_id=1, source_target_pairs={{0,8},{8,16},{16,24},{24,32},{32,40},{40,48},{48,56},{56,64},{64,7... | collective-permute-start | bytes 8847368 | tf_op jit(solution)/shard_map/ppermute | solution.py:24
  120.9 7.5 %collective-permute-start.5 = (s32[1920]{0:T(1024)S(1)}, s32[1920]{0:T(1024)S(1)}, u32[]{:S(2)}, u32[]{:S(2)}) collective-permute-start(s32[1920]{0:T(1024)S(1)} %collective-permute-done.4), channel_id=1, source_target_pairs={{0,7},{1,0},{2,1},{3,2},{4,3},{5,4},{6,5},{7,6},{8,15},{9,8},{10,9... | collective-permute-start | bytes 23048 | tf_op jit(solution)/shard_map/ppermute | solution.py:24
  142.1 66.3 %collective-permute-start.7 = (bf16[1920,768]{1,0:T(8,128)(2,1)S(1)}, bf16[1920,768]{1,0:T(8,128)(2,1)S(1)}, u32[]{:S(2)}, u32[]{:S(2)}) collective-permute-start(bf16[1920,768]{1,0:T(8,128)(2,1)S(1)} %collective-permute-done.6), channel_id=1, source_target_pairs={{0,7},{1,0},{2,1},{3,2},{4,3},{5,4},{6,5},{7,6},{8,15},{9,8},{10,9... | collective-permute-start | bytes 8847368 | tf_op jit(solution)/shard_map/ppermute | solution.py:24
where the time goes:
time: 220 us; the launch traced here: 219 us
  waiting for transfers between devices  180 us (82%)
  matrix products  33.1 us (15%)
  starting transfers between devices  3.08 us (1%)
    ppermute x8, waiting for transfers between devices, shifted(): return lax.ppermute(value, axis, pairs)  180 us
    dot_general x3, matrix products, tally(): lax.dot_general(query, cand, (((1,), (1,)), ((), ())), preferred_element_...  33.1 us
  transfers between devices with their start and end apart: 8, of which 6 were waited for; matrix products, arithmetic and copies ran while one was open for 11% of the time, Pallas kernels for 0%

commit v1 on v0

v1 whole, which is shorter than its diff:
```python
import jax
import jax.numpy as jnp
from jax import lax
from jax.experimental import pallas as pl
from jax.experimental.pallas import tpu as pltpu
from jax.sharding import PartitionSpec as P

MESH = pl.DeviceIdType.MESH
THRESHOLD = 0.6
SHARPNESS = 0.05
LOG2E = 1.4426950408889634

PARTS = 1
RELAYS = 2
PIECE = 48
GROUP = PARTS * PIECE
TILE = 384
AHEAD = 4
LAG_R, LAG_H, LAG_B, LAG_Z, LAG_D = (2, 4), 7, 10, 13, 14

SENDS = [
    0, 25, 1, 27, 16, 10, 18, 11, 8, 1, 26, 2, 59, 17, 11, 19,
    1, 9, 2, 27, 16, 58, 18, 8, 24, 2, 10, 3, 11, 17, 57, 19,
    2, 25, 3, 11, 0, 8, 18, 56, 24, 3, 26, 0, 8, 1, 9, 19,
    3, 25, 0, 27, 16, 9, 2, 10, 24, 0, 26, 1, 9, 17, 10, 3,
    0, 25, 1, 27, 16, 10, 18, 11, 8, 1, 26, 2, 59, 17, 11, 19,
    1, 9, 2, 27, 16, 58, 18, 8, 24, 2, 10, 3, 11, 17, 57, 19,
    2, 25, 3, 11, 0, 8, 18, 56, 24, 3, 26, 0, 8, 1, 9, 19,
    3, 25, 0, 27, 16, 9, 2, 10, 24, 0, 26, 1, 9, 17, 10, 3,
    4, 29, 5, 31, 20, 14, 22, 15, 12, 5, 30, 6, 63, 21, 15, 23,
    5, 13, 6, 31, 20, 62, 22, 12, 28, 6, 14, 7, 15, 21, 61, 23,
    6, 29, 7, 15, 4, 12, 22, 60, 28, 7, 30, 4, 12, 5, 13, 23,
    7, 29, 4, 31, 20, 13, 6, 14, 28, 4, 30, 5, 13, 21, 14, 7,
    4, 29, 5, 31, 20, 14, 22, 15, 12, 5, 30, 6, 63, 21, 15, 23,
    5, 13, 6, 31, 20, 62, 22, 12, 28, 6, 14, 7, 15, 21, 61, 23,
    6, 29, 7, 15, 4, 12, 22, 60, 28, 7, 30, 4, 12, 5, 13, 23,
    7, 29, 4, 31, 20, 13, 6, 14, 28, 4, 30, 5, 13, 21, 14, 7,
]
RELAYED = [
    17, 0, 25, 0, 74752, 65, 0, 449, 0, 25, 0, 1, 0, 0, 73, 82944,
    25, 0, 1, 0, 0, 0, 91136, 81, 0, 1, 0, 9, 73, 66560, 0, 0,
    0, 0, 9, 0, 74752, 81, 0, 0, 0, 0, 0, 17, 473, 0, 89, 82944,
    9, 0, 0, 0, 0, 465, 91136, 65, 0, 17, 0, 0, 89, 66560, 457, 0,
    17, 0, 25, 0, 74752, 65, 0, 449, 0, 25, 0, 1, 0, 0, 73, 82944,
    25, 0, 1, 0, 0, 0, 91136, 81, 0, 1, 0, 9, 73, 66560, 0, 0,
    0, 0, 9, 0, 74752, 81, 0, 0, 0, 0, 0, 17, 473, 0, 89, 82944,
    9, 0, 0, 0, 0, 465, 91136, 65, 0, 17, 0, 0, 89, 66560, 457, 0,
    49, 0, 57, 0, 107520, 97, 0, 481, 0, 57, 0, 33, 0, 0, 105, 115712,
    57, 0, 33, 0, 0, 0, 123904, 113, 0, 33, 0, 41, 105, 99328, 0, 0,
    0, 0, 41, 0, 107520, 113, 0, 0, 0, 0, 0, 49, 505, 0, 121, 115712,
    41, 0, 0, 0, 0, 497, 123904, 97, 0, 49, 0, 0, 121, 99328, 489, 0,
    49, 0, 57, 0, 107520, 97, 0, 481, 0, 57, 0, 33, 0, 0, 105, 115712,
    57, 0, 33, 0, 0, 0, 123904, 113, 0, 33, 0, 41, 105, 99328, 0, 0,
    0, 0, 41, 0, 107520, 113, 0, 0, 0, 0, 0, 49, 505, 0, 121, 115712,
    41, 0, 0, 0, 0, 497, 123904, 97, 0, 49, 0, 0, 121, 99328, 489, 0,
]
HOMES = [
    16, 530, 84, 598, 177, 691, 245, 759, 512, 66, 580, 134, 673, 227, 741, 39,
    64, 578, 132, 646, 225, 739, 37, 551, 576, 130, 644, 198, 737, 35, 549, 103,
    128, 642, 196, 710, 33, 547, 101, 615, 640, 194, 708, 6, 545, 99, 613, 167,
    192, 706, 4, 518, 97, 611, 165, 679, 704, 2, 516, 70, 609, 163, 677, 231,
    0, 514, 68, 582, 161, 675, 229, 743, 512, 66, 580, 134, 673, 227, 741, 39,
    64, 578, 132, 646, 225, 739, 37, 551, 576, 130, 644, 198, 737, 35, 549, 103,
    128, 642, 196, 710, 33, 547, 101, 615, 640, 194, 708, 6, 545, 99, 613, 167,
    192, 706, 4, 518, 97, 611, 165, 679, 720, 18, 532, 86, 625, 179, 693, 247,
    264, 778, 332, 846, 425, 939, 493, 1007, 792, 346, 860, 414, 953, 507, 1021, 319,
    344, 858, 412, 926, 505, 1019, 317, 831, 856, 410, 924, 478, 1017, 315, 829, 383,
    408, 922, 476, 990, 313, 827, 381, 895, 920, 474, 988, 286, 825, 379, 893, 447,
    472, 986, 284, 798, 377, 891, 445, 959, 984, 282, 796, 350, 889, 443, 957, 511,
    280, 794, 348, 862, 441, 955, 509, 1023, 792, 346, 860, 414, 953, 507, 1021, 319,
    344, 858, 412, 926, 505, 1019, 317, 831, 856, 410, 924, 478, 1017, 315, 829, 383,
    408, 922, 476, 990, 313, 827, 381, 895, 920, 474, 988, 286, 825, 379, 893, 447,
    472, 986, 284, 798, 377, 891, 445, 959, 968, 266, 780, 334, 873, 427, 941, 495,
]


def lookup(index):
    words = [jnp.int32(0)] * 3
    for i in range(len(SENDS)):
        hit = index == i
        words = [jnp.where(hit, jnp.int32(t[i]), w) for t, w in zip((SENDS, RELAYED, HOMES), words)]
    return words


def bits(word, low, count):
    return (word // (1 << low)) % (1 << count)


def device(position, z, core):
    x, y = position % 4, position // 4
    return ((y % 2) * 16 + z * 2 + core, (y // 2) * 4 + x)


def kernel(
    emb, valid, best_out, count_out, data, relay, bounce, id_0, id_1, id_own, id_way, weight, acc_best, acc_count, sent, got,
    own_ss, relay_ss, z_ss, b_ss, d_ss, v_ss, s_ss, home_rs, relay_rs, z_rs, b_rs, d_rs, v_rs, s_rs, load_sem, vload_sem,
):
    members = emb.shape[0]
    groups = members // GROUP
    HOME, Z, D, OWN = 0, 1, 2, 3
    row, col = lax.axis_index("row"), lax.axis_index("col")
    core = row % 2
    z = (row // 2) % 8
    here = ((col // 4) * 2 + row // 16) * 4 + col % 4

    load = pltpu.make_async_copy(emb, data.at[OWN], load_sem)
    load.start()
    vload = pltpu.make_async_copy(valid, id_own, vload_sem)
    vload.start()

    barrier = pltpu.get_barrier_semaphore()
    position = ((col // 4) * 2 + row // 16) * 4 + col % 4
    across = position + 4 - 8 * ((position // 4) % 2)
    friends = [(row + 1 - 2 * core, col)]
    friends += [device((position + i) % 16, z, core) for i in range(1, 16)]
    friends += [device(at, (z + i) % 8, core) for i in (1, 2, 6, 7) for at in (position, across)]
    for friend in friends:
        pl.semaphore_signal(barrier, inc=1, device_id=friend, device_id_type=MESH)
    sends, relayed, homes = lookup(row * 8 + col)
    pl.semaphore_wait(barrier, len(friends))

    part_pos = [bits(sends, 7 * p, 4) for p in range(PARTS)]
    part_rel = [bits(sends, 7 * p + 4, 1) == 1 for p in range(PARTS)]
    part_slot = [bits(sends, 7 * p + 5, 2) for p in range(PARTS)]
    part_local = [jnp.logical_and(jnp.logical_not(part_rel[p]), part_pos[p] == here) for p in range(PARTS)]
    part_home = [jnp.logical_and(jnp.logical_not(part_rel[p]), part_pos[p] != here) for p in range(PARTS)]
    slot_on = [bits(relayed, 10 * r, 1) == 1 for r in range(RELAYS)]
    slot_part = [bits(relayed, 10 * r + 1, 2) for r in range(RELAYS)]
    slot_pos = [bits(relayed, 10 * r + 3, 4) for r in range(RELAYS)]
    slot_again = [bits(relayed, 10 * r + 7, 1) == 1 for r in range(RELAYS)]
    chain = bits(homes, 0, 3)
    held_row = bits(homes, 3, 1) * 16 + z * 2 + core
    z_next = (z + 7 + 2 * core) % 8
    z_dev = device(bits(homes, 4, 2) * 4 + col % 4, z_next, core)
    sibling = (row + 1 - 2 * core, col)
    v_pos = bits(homes, 6, 4)
    origin_b = (held_row, (chain - held_row + 64) % 8)
    q_row = (held_row + 2 * (1 - core)) % 32
    origin_a = (q_row, (chain - q_row + 64) % 8)

    def rows(piece):
        return pl.ds(pl.multiple_of(piece * PIECE, PIECE), PIECE)

    def grows(group):
        return pl.ds(pl.multiple_of(group * GROUP, GROUP), GROUP)

    def remote(src, dst, ss, rs, dev):
        return pltpu.make_async_remote_copy(
            src_ref=src, dst_ref=dst, send_sem=ss, recv_sem=rs, device_id=dev, device_id_type=MESH
        )

    def own_send(g):
        for p in range(PARTS):
            piece = g * PARTS + p
            dev = device(part_pos[p], z, core)

            @pl.when(part_local[p])
            def _():
                pltpu.make_async_copy(emb.at[rows(piece)], data.at[HOME, rows(piece)], home_rs.at[piece]).start()

            @pl.when(part_home[p])
            def _():
                remote(emb.at[rows(piece)], data.at[HOME, rows(piece)], own_ss.at[p], home_rs.at[piece], dev).start()

            @pl.when(part_rel[p])
            def _():
                remote(
                    emb.at[rows(piece)], relay.at[part_slot[p], rows(g)], own_ss.at[p],
                    relay_rs.at[part_slot[p], g], dev,
                ).start()

    def relay_send(r, g):
        @pl.when(slot_on[r])
        def _():
            piece = g * PARTS + slot_part[r]
            src = relay.at[r, rows(g)]
            dev = device(slot_pos[r], z, core)
            remote(src, src, relay_ss.at[r], relay_rs.at[r, g], sibling).wait_recv()
            if r + 1 < RELAYS:

                @pl.when(slot_again[r])
                def _():
                    remote(src, relay.at[r + 1, rows(g)], relay_ss.at[r], relay_rs.at[r + 1, g], dev).start()

            @pl.when(jnp.logical_not(slot_again[r]))
            def _():
                remote(src, data.at[HOME, rows(piece)], relay_ss.at[r], home_rs.at[piece], dev).start()

    way = 2 * core - 1
    wraps = z == 7 * core
    bounces = z == 6 - 5 * core
    far_dev = device(bits(homes, 4, 2) * 4 + col % 4, (z_next + way + 8) % 8, core)
    near_dev = device(here, (z - way + 8) % 8, core)

    def z_copy(g):
        return remote(data.at[HOME, grows(g)], data.at[Z, grows(g)], z_ss, z_rs.at[g], z_dev)

    def z_send(g):
        far = jnp.logical_and(wraps, g % 2 == 1)

        @pl.when(far)
        def _():
            remote(data.at[HOME, grows(g)], bounce.at[grows(g // 2)], z_ss, b_rs.at[g // 2], far_dev).start()

        @pl.when(jnp.logical_not(far))
        def _():
            z_copy(g).start()

    def bounce_copy(g):
        return remote(bounce.at[grows(g // 2)], data.at[Z, grows(g)], b_ss, z_rs.at[g], near_dev)

    def bounce_step(g):
        @pl.when(jnp.logical_and(bounces, g % 2 == 1))
        def _():
            src = bounce.at[grows(g // 2)]
            remote(src, src, b_ss, b_rs.at[g // 2], sibling).wait_recv()
            bounce_copy(g).start()

    def d_copy(g, slot):
        return remote(data.at[slot, grows(g)], data.at[D, grows(g)], d_ss, d_rs.at[g], sibling)

    def home_step(g):
        for p in range(PARTS):
            piece = g * PARTS + p
            remote(data.at[HOME, rows(piece)], data.at[HOME, rows(piece)], z_ss, home_rs.at[piece], sibling).wait_recv()
        z_send(g)

        @pl.when(core == 0)
        def _():
            d_copy(g, HOME).start()

    def z_step(g):
        z_copy(g).wait_recv()

        @pl.when(core == 1)
        def _():
            d_copy(g, Z).start()

    for g in range(AHEAD):
        own_send(g)

    v_here = v_pos == here
    for t, target in enumerate((id_0, id_way)):

        @pl.when(jnp.logical_and(core == t, v_here))
        def _():
            pltpu.make_async_copy(valid, target, v_rs.at[2 * t]).start()

        @pl.when(jnp.logical_and(core == t, jnp.logical_not(v_here)))
        def _():
            remote(valid, target, v_ss.at[0], v_rs.at[2 * t], device(v_pos, z, core)).start()

    v_on = remote(id_way, id_0, v_ss.at[1], v_rs.at[0], z_dev)
    v_over = remote(id_0, id_1, v_ss.at[2], v_rs.at[1], sibling)

    def v_step():
        @pl.when(core == 1)
        def _():
            remote(id_way, id_way, v_ss.at[0], v_rs.at[2], sibling).wait_recv()
            v_on.start()

    def v_share():
        v_on.wait_recv()
        v_over.start()

    acc_best[...] = jnp.full(acc_best.shape, -1.0, jnp.float32)
    acc_count[...] = jnp.zeros(acc_count.shape, jnp.float32)

    def spread(slot):
        line = (id_0, id_1, id_own)[slot]
        for i in range(members // 128):
            part = line[i * 128 : (i + 1) * 128].astype(jnp.float32).reshape(1, 128)
            weight[slot, i * 128 : (i + 1) * 128, :] = jnp.broadcast_to(part, (128, 128)).T

    def tiles_of(jobs):
        found = []
        for unit, c_slot, q_slot, c, q, own in jobs:
            c_at = pl.ds(pl.multiple_of(c * TILE, TILE), TILE)
            q_at = pl.ds(pl.multiple_of(q * TILE, TILE), TILE)
            scores = lax.dot_general(
                data[c_slot, c_at, :], data[q_slot, q_at, :], (((1,), (1,)), ((), ())), preferred_element_type=jnp.float32
            )
            w = weight[unit, c_at, :]
            allowed = jnp.concatenate([w] * (TILE // 128), axis=1) > 0.5
            if own:
                shape = (TILE, TILE)
                differ = lax.broadcasted_iota(jnp.int32, shape, 0) != lax.broadcasted_iota(jnp.int32, shape, 1)
                allowed = jnp.logical_and(allowed, differ)
            top = jnp.where(allowed, scores, -1.0).reshape(TILE // 8, 8, TILE)
            soft = 1.0 / (1.0 + jnp.exp2(scores * (-LOG2E / SHARPNESS) + THRESHOLD * LOG2E / SHARPNESS))
            soft = jnp.where(allowed, soft, 0.0).reshape(TILE // 8, 8, TILE)
            found.append((unit, q_at, jnp.max(top, axis=0), jnp.sum(soft, axis=0)))
        for unit, q_at, top, soft in found:
            acc_best[unit, :, q_at] = jnp.maximum(acc_best[unit, :, q_at], top)
            acc_count[unit, :, q_at] = acc_count[unit, :, q_at] + soft

    load.wait()
    vload.wait()
    spread(2)

    tiles = members // TILE
    lag = LAG_D

    def own_tiles(n):
        q = n % tiles

        @pl.when(n < tiles)
        def _():
            tiles_of([(2, OWN, OWN, q, q, True)])

        @pl.when(n >= tiles)
        def _():
            tiles_of([(2, OWN, OWN, (q + n // tiles) % tiles, q, False)])

    def pair_tiles(t, first, last):
        @pl.loop(first, last)
        def _(n):
            late = jnp.where(n <= t + 1, t, n - t - 2)
            held = jnp.where(n <= t + 1, n, t + 1)
            c = jnp.where(core == 0, held, late)
            q = jnp.where(core == 0, late, held)
            tiles_of([(0, core, 1 - core, c, q, False), (1, D, HOME, late, held, False)])

    per = TILE // GROUP

    @pl.loop(0, groups + lag)
    def _(s):
        for r in range(RELAYS):

            @pl.when(jnp.logical_and(s >= LAG_R[r], s < groups + LAG_R[r]))
            def _():
                relay_send(r, s - LAG_R[r])

        @pl.when(jnp.logical_and(s >= LAG_B, s < groups + LAG_B))
        def _():
            bounce_step(s - LAG_B)

        @pl.when(jnp.logical_and(s >= LAG_H, s < groups + LAG_H))
        def _():
            home_step(s - LAG_H)

        @pl.when(s + AHEAD < groups)
        def _():
            own_send(s + AHEAD)

        @pl.when(jnp.logical_and(s >= LAG_Z, s < groups + LAG_Z))
        def _():
            z_step(s - LAG_Z)

        @pl.when(s >= LAG_D)
        def _():
            d_copy(s - LAG_D, HOME).wait_recv()

        @pl.when(s < tiles * tiles)
        def _():
            own_tiles(s)

        @pl.when(s == LAG_H)
        def _():
            v_step()

        @pl.when(s == LAG_Z)
        def _():
            v_share()

        @pl.when(s == LAG_D)
        def _():
            v_over.wait_recv()
            for slot in range(2):
                spread(slot)

        done = s - lag + 1
        t = done // per - 1
        phase = done % per

        @pl.when(t >= 0)
        def _():
            total = jnp.where(t == tiles - 1, tiles, 2 * t + 2)
            pair_tiles(t, total * phase // per, jnp.where(t == tiles - 1, total, total * (phase + 1) // per))

    def folded(unit):
        return (
            jnp.max(acc_best[unit], axis=0, keepdims=True),
            jnp.sum(acc_count[unit], axis=0, keepdims=True),
        )

    for unit in range(2):
        b, n = folded(unit)
        sent[unit, 0:1, :] = b
        sent[unit, 1:2, :] = n
    mine_b, mine_n = folded(2)

    s_dev = [origin_a, origin_b]
    s_copies = [remote(sent.at[u], got.at[u], s_ss.at[u], s_rs.at[u], s_dev[u]) for u in range(2)]
    s_here = [jnp.logical_and(d[0] == row, d[1] == col) for d in s_dev]
    for u in range(2):

        @pl.when(s_here[u])
        def _():
            got[u] = sent[u]

        @pl.when(jnp.logical_not(s_here[u]))
        def _():
            s_copies[u].start()

    z_all = remote(data.at[HOME], data.at[Z], z_ss, z_rs.at[0], z_dev)
    z_all.wait_send()

    @pl.when(bounces)
    def _():
        half = pl.ds(0, groups // 2 * GROUP)
        remote(bounce.at[half], data.at[Z, half], b_ss, z_rs.at[0], near_dev).wait_send()

    remote(data.at[HOME], data.at[D], d_ss, d_rs.at[0], sibling).wait_send()
    part_rows = pl.ds(0, members // PARTS)
    for p in range(PARTS):

        @pl.when(jnp.logical_not(part_local[p]))
        def _():
            remote(emb.at[part_rows], data.at[HOME, part_rows], own_ss.at[p], home_rs.at[0], sibling).wait_send()

    for r in range(RELAYS):

        @pl.when(slot_on[r])
        def _():
            remote(relay.at[r], data.at[HOME, part_rows], relay_ss.at[r], home_rs.at[0], sibling).wait_send()

    @pl.when(jnp.logical_not(v_here))
    def _():
        remote(valid, id_0, v_ss.at[0], v_rs.at[0], sibling).wait_send()

    @pl.when(core == 1)
    def _():
        v_on.wait_send()

    v_over.wait_send()

    for u in range(2):

        @pl.when(jnp.logical_not(s_here[u]))
        def _():
            s_copies[u].wait_send()
            s_copies[u].wait_recv()

    best_out[...] = jnp.maximum(mine_b, jnp.maximum(got[0, 0:1, :], got[1, 0:1, :]))[0]
    count_out[...] = (mine_n + got[0, 1:2, :] + got[1, 1:2, :])[0]


def shards(embeddings, valid):
    members, width = embeddings.shape
    groups = members // GROUP
    dma = pltpu.SemaphoreType.DMA
    best, count = pl.pallas_call(
        kernel,
        out_shape=[jax.ShapeDtypeStruct((members,), jnp.float32)] * 2,
        in_specs=[pl.BlockSpec(memory_space=pl.ANY)] * 2,
        out_specs=[pl.BlockSpec(memory_space=pltpu.VMEM)] * 2,
        scratch_shapes=[
            pltpu.VMEM((4, members, width), jnp.bfloat16),
            pltpu.VMEM((RELAYS, members // PARTS, width), jnp.bfloat16),
            pltpu.VMEM((groups // 2 * GROUP, width), jnp.bfloat16),
            pltpu.VMEM((members,), jnp.int32),
            pltpu.VMEM((members,), jnp.int32),
            pltpu.VMEM((members,), jnp.int32),
            pltpu.VMEM((members,), jnp.int32),
            pltpu.VMEM((3, members, 128), jnp.float32),
            pltpu.VMEM((3, 8, members), jnp.float32),
            pltpu.VMEM((3, 8, members), jnp.float32),
            pltpu.VMEM((3, 2, members), jnp.float32),
            pltpu.VMEM((3, 2, members), jnp.float32),
            dma((PARTS,)),
            dma((RELAYS,)),
            dma,
            dma,
            dma,
            dma((3,)),
            dma((2,)),
            dma((groups * PARTS,)),
            dma((RELAYS, groups)),
            dma((groups,)),
            dma((groups // 2,)),
            dma((groups,)),
            dma((3,)),
            dma((2,)),
            dma,
            dma,
        ],
        compiler_params=pltpu.CompilerParams(collective_id=0, has_side_effects=True, vmem_limit_bytes=60 * 2**20),
    )(embeddings, valid)
    return best, count


def solution(mesh):
    return jax.shard_map(
        shards,
        mesh=mesh,
        in_specs=(P(("row", "col"), None), P(("row", "col"))),
        out_specs=(P(("row", "col")), P(("row", "col"))),
        check_vma=False,
    )
```

time: 220 us -> 90.2 us (0.41)
  waiting for transfers between devices: 180 us -> 0 us
  Pallas kernels: 0 us -> 86.7 us
  matrix products: 33.1 us -> 0 us
  starting transfers between devices: 3.08 us -> 0 us
  local copies, waits for them, and re-layouts: 0.01 us -> 2.59 us
    ppermute x8 -> x0, waiting for transfers between devices: 180 us -> none  [shifted(): return lax.ppermute(value, axis, pairs)]
    pallas_call x0 -> x1, Pallas kernels: none -> 86.7 us  [shards(): pl.pallas_call(kernel, out_shape=[jax.ShapeDtypeStruct((members,), jnp.fl...]
    dot_general x3 -> x0, matrix products: 33.1 us -> none  [tally(): lax.dot_general(query, cand, (((1,), (1,)), ((), ())), preferred_element_...]
    ppermute x8 -> x0, starting transfers between devices: 3.08 us -> none  [shifted(): return lax.ppermute(value, axis, pairs)]
    unnamed x2, local copies, waits for them, and re-layouts: 0.01 us -> 2.59 us
  transfers between devices with their start and end apart: 8 -> 0, of which waited for: 6 -> 0; matrix products, arithmetic and copies ran while one was open for 11% -> 0% of each run, Pallas kernels for 0% -> 0%
where the time goes in v1:
time: 90.2 us; the launch traced here: 89.9 us
  Pallas kernels  86.7 us (96%)
  local copies, waits for them, and re-layouts  2.59 us (3%)
    pallas_call x1, Pallas kernels, shards(): pl.pallas_call(kernel, out_shape=[jax.ShapeDtypeStruct((members,), jnp.fl...  86.7 us
    unnamed x2, local copies, waits for them, and re-layouts  2.59 us

profile of v1, /device:TPU:6, one launch (start us, length us, event | category | flops | bytes accessed | tf_op | source)
XLA Modules:
  0.0 89.9 jit_solution(15119178705981606768)
XLA Ops:
  0.6 86.7 %shard_map.41 = (f32[1920]{0:T(1024)}, f32[1920]{0:T(1024)}) custom-call(bf16[1920,768]{1,0:T(8,128)(2,1)} %emb.1, s32[1920]{0:T(1024)} %valid.1), custom_call_target="tpu_custom_call" | custom-call | tf_op jit(solution)/shard_map/pallas_call | solution.py:453
  87.3 1.3 %copy.6 = f32[1920]{0:T(1024)} copy(f32[1920]{0:T(1024)} %get-tuple-element.4) | data formatting | bytes 15360
  88.6 1.3 %copy.7 = f32[1920]{0:T(1024)} copy(f32[1920]{0:T(1024)} %get-tuple-element.5) | data formatting | bytes 15360
